TPU v7x, 256 devices: a whole 4x4x8 slice. The times are simulated.
256 devices in a mesh: client: 16 (over y_lo, z), tensor: 8 (over x, core), sdata: 2 (over y_hi).
Axes of the slice: x: 4, y: 4 (y_hi: 2, y_lo: 2; y = y_hi * 2 + y_lo), z: 8, core: 2. Of those that a mesh axis runs over, the one named last changes fastest.
Arguments:
- client_input: bfloat16 [12288, 2048], P(('client', 'sdata')), may hold values from -6 to 6
- client_gain: bfloat16 [16, 2048], P('client'), may hold values from 0.5 to 1.5
- query_weight: bfloat16 [16, 2048, 2048], P('client', None, 'tensor'), as said below
- key_weight: bfloat16 [16, 2048, 512], P('client', None, 'tensor'), as said below
- client_value_weight: bfloat16 [16, 2048, 512], P('client', None, 'tensor'), may hold values from -0.125 to 0.125
- output_weight: bfloat16 [16, 2048, 2048], P('client', None, 'tensor'), may hold values from -0.125 to 0.125
- server_gain: bfloat16 [2, 2048], P('sdata'), may hold values from 0.5 to 1.5
- server_gate: bfloat16 [2, 2048, 4096], P('sdata', None, 'tensor'), may hold values from -0.125 to 0.125
- server_up: bfloat16 [2, 2048, 4096], P('sdata', None, 'tensor'), may hold values from -0.125 to 0.125
- server_down: bfloat16 [2, 4096, 2048], P('sdata', 'tensor'), may hold values from -0.09375 to 0.09375
- upstream: bfloat16 [12288, 2048], P(('client', 'sdata')), may hold values from -6 to 6
- assignment: int32 [16], replicated, may hold values from 0 to 1, as said below
Outputs:
- query_update: bfloat16 [2048, 2048], P(('client', 'sdata'), 'tensor')
- key_update: bfloat16 [2048, 512], P(('client', 'sdata'), 'tensor')
- value_update: bfloat16 [2048, 512], P(('client', 'sdata'), 'tensor')
- output_update: bfloat16 [2048, 2048], P(('client', 'sdata'), 'tensor')
Inputs may be any that keep to these rules, and one draw needn't show every extreme that they name: `assignment`: each of the 2 server groups is named by exactly 8 clients. `query_weight`: independent entries with a spread of about 2048 ** -0.5. `key_weight`: entries with a spread of about 2048 ** -0.5 or more.
All inputs are finite; a program needn't handle non-finite values.
Results may differ from a plain program's by a relative error of at most 0.038.
The roundings to bfloat16 on the way count: a program that leaves them out, or rounds other values in their place, can miss the bound.
Values may be sent and summed in bfloat16 or wider, within the bound.
No kernel may reach another device: no remote copies, remote signals or barrier semaphores. Data moves between devices by JAX's collectives and lax.ppermute only.
A program may use at most 128 MiB of HBM per device.

v0:
```python
from functools import partial
import math
import jax
import jax.numpy as jnp
from jax import lax
from jax.sharding import PartitionSpec as P

HEAD_DIM = 64


def cut_along(value, dim, length):
    before, after = (value.shape[:dim], value.shape[dim + 1 :])
    return jnp.moveaxis(value.reshape(*before, length, -1, *after), dim, 0)


def sum_at_owner(value, axis, dim):
    length = lax.axis_size(axis)
    tiles = lax.all_to_all(cut_along(value, dim, length), axis, 0, 0, tiled=True)
    return jnp.sum(tiles.astype(jnp.float32), axis=0)


def rotary_tables(length):
    halfway = HEAD_DIM // 2
    positions = jnp.arange(length).astype(jnp.float32)
    exponents = jnp.arange(halfway).astype(jnp.float32) * (2.0 / HEAD_DIM)
    frequencies = jnp.exp(-math.log(500000.0) * exponents)
    angles = positions[:, None] * frequencies[None, :]
    cosine_table = jnp.concatenate([jnp.cos(angles), jnp.cos(angles)], 1)
    sine_table = jnp.concatenate([jnp.sin(angles), jnp.sin(angles)], 1)
    return (cosine_table, sine_table)


def rotary(heads_in, cosine_table, sine_table):
    halfway = heads_in.shape[-1] // 2
    turned = jnp.concatenate([-heads_in[..., halfway:], heads_in[..., :halfway]], -1)
    return heads_in * cosine_table[:, None, :] + turned * sine_table[:, None, :]


def normalize(rows_in, gain):
    rows_float = rows_in.astype(jnp.float32)
    inv_rms = lax.rsqrt(jnp.mean(rows_float * rows_float, -1, keepdims=True) + 1e-05)
    return (rows_float * inv_rms * gain.astype(jnp.float32)).astype(jnp.bfloat16)


def attention_part(normed, query_matrix, client_key_matrix, value_matrix, output_matrix):
    length = normed.shape[0]
    query_count = query_matrix.shape[1] // HEAD_DIM
    shared_count = client_key_matrix.shape[1] // HEAD_DIM
    group_size = query_count // shared_count
    cosine_table, sine_table = rotary_tables(length)
    queries = jnp.dot(normed, query_matrix, preferred_element_type=jnp.float32).reshape(
        length, query_count, HEAD_DIM
    )
    queries = (
        rotary(queries, cosine_table, sine_table)
        .astype(jnp.bfloat16)
        .reshape(length, shared_count, group_size, HEAD_DIM)
    )
    key_heads = jnp.dot(normed, client_key_matrix, preferred_element_type=jnp.float32).reshape(
        length, shared_count, HEAD_DIM
    )
    key_heads = rotary(key_heads, cosine_table, sine_table).astype(jnp.bfloat16)
    value_heads = (
        jnp.dot(normed, value_matrix, preferred_element_type=jnp.float32)
        .astype(jnp.bfloat16)
        .reshape(length, shared_count, HEAD_DIM)
    )
    scores = jnp.einsum(
        "qgrd,kgd->grqk", queries.astype(jnp.float32), key_heads.astype(jnp.float32)
    ) * HEAD_DIM ** (-0.5)
    row_ids = lax.broadcasted_iota(jnp.int32, (length, length), 0)
    col_ids = lax.broadcasted_iota(jnp.int32, (length, length), 1)
    scores = jnp.where(col_ids <= row_ids, scores, -1e30)
    highest = lax.stop_gradient(jnp.max(scores, -1, keepdims=True))
    exponent = jnp.exp(scores - highest)
    weights = (exponent / jnp.sum(exponent, -1, keepdims=True)).astype(jnp.bfloat16)
    context = jnp.einsum(
        "grqk,kgd->qgrd", weights.astype(jnp.float32), value_heads.astype(jnp.float32)
    )
    context = context.astype(jnp.bfloat16).reshape(length, query_count * HEAD_DIM)
    return lax.dot_general(
        context, output_matrix, (((1,), (1,)), ((), ())), preferred_element_type=jnp.float32
    )


def server_pull(rows_in, upstream_rows, gain, gate_matrix, up_matrix, down_matrix):
    rows_float = rows_in.astype(jnp.float32)
    inv_rms = lax.rsqrt(jnp.mean(rows_float * rows_float, -1, keepdims=True) + 1e-05)
    gain_float = gain.astype(jnp.float32)
    server_normed = (rows_float * inv_rms * gain_float).astype(jnp.bfloat16)
    gate_value = jnp.dot(server_normed, gate_matrix, preferred_element_type=jnp.float32)
    up_value = jnp.dot(server_normed, up_matrix, preferred_element_type=jnp.float32)
    pulled = lax.dot_general(
        upstream_rows, down_matrix, (((1,), (1,)), ((), ())), preferred_element_type=jnp.float32
    )
    sigmoid_gate = jax.nn.sigmoid(gate_value)
    gate_grad = (
        pulled * up_value * sigmoid_gate * (1.0 + gate_value * (1.0 - sigmoid_gate))
    ).astype(jnp.bfloat16)
    up_grad = (pulled * gate_value * sigmoid_gate).astype(jnp.bfloat16)
    normed_grad = lax.dot_general(
        gate_grad, gate_matrix, (((1,), (1,)), ((), ())), preferred_element_type=jnp.float32
    )
    normed_grad = normed_grad + lax.dot_general(
        up_grad, up_matrix, (((1,), (1,)), ((), ())), preferred_element_type=jnp.float32
    )
    weighted = normed_grad * gain_float
    return inv_rms * weighted - rows_float * inv_rms**3 * jnp.mean(
        weighted * rows_float, -1, keepdims=True
    )


def over_clients(pieces):
    return lax.all_to_all(pieces, "client", split_axis=1, concat_axis=1, tiled=True)


def over_groups(pieces):
    return lax.all_to_all(pieces, "sdata", split_axis=1, concat_axis=1, tiled=True)


def relay_out(stacked, group_order, client_count):
    count_rows, length, breadth = stacked.shape
    pieces = stacked.reshape(count_rows, client_count, length // client_count, breadth)
    arrived = jnp.take(over_clients(pieces), group_order, axis=1)
    return over_groups(arrived).reshape(count_rows, length, breadth)


def relay_back(stacked, inverse, client_count):
    count_rows, length, breadth = stacked.shape
    pieces = stacked.reshape(count_rows, client_count, length // client_count, breadth)
    arrived = jnp.take(over_groups(pieces), inverse, axis=1)
    return over_clients(arrived).reshape(count_rows, length, breadth)


def share_sum(partial_rows):
    return sum_at_owner(partial_rows.astype(jnp.bfloat16), "tensor", 1)


def widen_rows(stacked):
    return lax.all_gather(stacked, "tensor", axis=2, tiled=True)


def local(
    client_input,
    client_gain,
    query_weight,
    key_weight,
    client_value_weight,
    output_weight,
    server_gain,
    server_gate,
    server_up,
    server_down,
    upstream,
    assignment,
):
    client_count = lax.axis_size("client")
    normed = normalize(client_input, client_gain[0])
    attended, pullback = jax.vjp(
        partial(attention_part, normed),
        query_weight[0],
        key_weight[0],
        client_value_weight[0],
        output_weight[0],
    )
    group_order = jnp.argsort(assignment, stable=True)
    inverse = jnp.argsort(group_order, stable=True)
    shard_width = client_input.shape[1] // lax.axis_size("tensor")
    shard_start = lax.axis_index("tensor") * shard_width
    own_input = lax.dynamic_slice_in_dim(client_input, shard_start, shard_width, 1)
    own_upstream = lax.dynamic_slice_in_dim(upstream, shard_start, shard_width, 1)
    cut_input = (own_input.astype(jnp.float32) + share_sum(attended)).astype(jnp.bfloat16)
    arrived = relay_out(jnp.stack([cut_input, own_upstream]), group_order, client_count)
    widened = widen_rows(arrived)
    pulled = server_pull(
        widened[0], widened[1], server_gain[0], server_gate[0], server_up[0], server_down[0]
    )
    cut_grad = (share_sum(pulled) + arrived[1].astype(jnp.float32)).astype(jnp.bfloat16)
    returned = relay_back(cut_grad[None], inverse, client_count)
    arriving_grad = widen_rows(returned)[0]
    query_grad, key_grad, value_grad, output_grad = pullback(arriving_grad.astype(jnp.float32))
    query_width = query_grad.shape[1]
    key_width = key_grad.shape[1]
    joined_grads = jnp.concatenate(
        [
            query_grad.astype(jnp.float32),
            key_grad.astype(jnp.float32),
            value_grad.astype(jnp.float32),
            output_grad.astype(jnp.float32),
        ],
        1,
    )
    summed = sum_at_owner(joined_grads.astype(jnp.bfloat16), ("client", "sdata"), 0) / client_count
    query_update = summed[:, :query_width].astype(jnp.bfloat16)
    key_update = summed[:, query_width : query_width + key_width].astype(jnp.bfloat16)
    value_update = summed[:, query_width + key_width : query_width + 2 * key_width].astype(
        jnp.bfloat16
    )
    output_update = summed[:, query_width + 2 * key_width :].astype(jnp.bfloat16)
    return (query_update, key_update, value_update, output_update)


def solution(mesh):
    placed = (
        P(("client", "sdata"), None),
        P("client", None),
        P("client", None, "tensor"),
        P("client", None, "tensor"),
        P("client", None, "tensor"),
        P("client", None, "tensor"),
        P("sdata", None),
        P("sdata", None, "tensor"),
        P("sdata", None, "tensor"),
        P("sdata", "tensor", None),
        P(("client", "sdata"), None),
        P(),
    )
    return jax.shard_map(
        local,
        mesh=mesh,
        in_specs=placed,
        out_specs=(
            P(("client", "sdata"), "tensor"),
            P(("client", "sdata"), "tensor"),
            P(("client", "sdata"), "tensor"),
            P(("client", "sdata"), "tensor"),
        ),
        check_vma=False,
    )
```

profile of v0, /device:TPU:4, one launch (start us, length us, event | category | flops | bytes accessed | tf_op | source)
XLA Modules:
  0.0 317.1 jit_solution(7294213297382398546)
XLA Ops:
  7.3 0.8 mul.298
  8.1 1.9 fusion.3
  10.0 2.1 fusion.91
  12.2 1.4 copy.27
  13.6 2.6 fusion.36
  19.8 0.8 fusion.54
  21.9 1.2 copy.46
  23.1 6.4 %all-to-all-start = ((bf16[8,384,256]{2,1,0:T(8,128)(2,1)}), bf16[8,384,256]{2,1,0:T(8,128)(2,1)}, u32[]{:S(2)}, u32[]{:S(2)}) async-start(bf16[8,384,256]{2,1,0:T(8,128)(2,1)} %bitcast.249), calls=%async_computation | async-start | bytes 3145728 | tf_op jit(solution)/shard_map/all_to_all | solution.py:18
  29.6 1.0 constant_dynamic-slice_fusion
  30.5 17.5 %all-to-all-done = bf16[8,384,256]{2,1,0:T(8,128)(2,1)} async-done(((bf16[8,384,256]{2,1,0:T(8,128)(2,1)}), bf16[8,384,256]{2,1,0:T(8,128)(2,1)}, u32[]{:S(2)}, u32[]{:S(2)}) %all-to-all-start) | async-done | bytes 1572896 | tf_op jit(solution)/shard_map/all_to_all | solution.py:18
  48.1 1.7 convert_reduce_fusion.2
  49.7 1.0 add_convert_fusion.1
  50.7 0.8 pad_maximum_fusion.1
  51.5 8.0 %all-to-all-start.1 = ((bf16[2,16,24,256]{3,2,0,1:T(8,128)(2,1)}), bf16[2,16,24,256]{3,2,0,1:T(8,128)(2,1)S(1)}, u32[]{:S(2)}, u32[]{:S(2)}) async-start(bf16[2,16,24,256]{3,2,0,1:T(8,128)(2,1)} %pad_maximum_fusion.1), calls=%async_computation.1 | async-start | bytes 786432 | tf_op jit(solution)/shard_map/all_to_all | solution.py:114
  59.6 1.3 sort.31
  62.1 10.1 %all-to-all-done.1 = bf16[2,16,24,256]{3,2,0,1:T(8,128)(2,1)S(1)} async-done(((bf16[2,16,24,256]{3,2,0,1:T(8,128)(2,1)}), bf16[2,16,24,256]{3,2,0,1:T(8,128)(2,1)S(1)}, u32[]{:S(2)}, u32[]{:S(2)}) %all-to-all-start.1) | async-done | bytes 393248 | tf_op jit(solution)/shard_map/all_to_all | solution.py:114
  72.2 0.8 copy.30
  73.0 1.6 gather_fusion
  74.6 11.3 %all_to_all.35 = bf16[2,16,24,256]{3,2,0,1:T(8,128)(2,1)S(1)} all-to-all(bf16[2,16,24,256]{3,2,0,1:T(8,128)(2,1)S(1)} %select_bitcast_fusion), channel_id=1, replica_groups=mesh['client'=16,'tensor'=8,'sdata'=2] {'sdata'}, dimensions={1} | all-to-all | bytes 786432 | tf_op jit(solution)/shard_map/all_to_all | solution.py:118
  87.5 29.4 %all-gather.3.cloned.1.call-done = bf16[2,384,2048]{2,1,0:T(8,128)(2,1)} async-done(((bf16[2,384,256]{2,1,0:T(8,128)(2,1)}), bf16[2,384,2048]{2,1,0:T(8,128)(2,1)}) %all-gather.3.cloned.1.call-update) | async-done | bytes 3145744 | tf_op jit(solution)/shard_map/all_gather | solution.py:140
  116.9 1.8 fusion.6
  119.3 4.1 %fusion.29 = f32[384,512]{1,0:T(8,128)} fusion(bf16[1,512,2048]{2,1,0:T(8,128)(2,1)} %param.21, bf16[2,384,2048]{2,1,0:T(8,128)(2,1)} %all-gather.3.cloned.1.call-done), kind=kOutput, calls=%fused_computation.50 | convolution fusion | flops 805306368 | bytes 4456448 | tf_op jit(solution)/shard_map/dot_general | solution.py:93
  123.5 1.9 fusion.24
  125.4 6.3 %fusion.22 = f32[384,2048]{1,0:T(8,128)} fusion(bf16[1,2048,512]{2,1,0:T(8,128)(2,1)} %param.19, f32[384,512]{1,0:T(8,128)} %fusion.29, bf16[1,2048,512]{2,1,0:T(8,128)(2,1)S(1)} %copy-done, f32[384,512]{1,0:T(8,128)} %fusion.24, f32[2048]{0:T(1024)S(1)} %bitcast.271, f32[384]{0:T(512)} %copy-done.29, bf16[2,384,2048]{2,1,0:T(8,128)(2,1)} %all-gather.3.cloned.1.call-done), kind=kOutput, calls=%fused_computation.43 | convolution fusion | flops 1615724544 | bytes 10496000 | tf_op jit(solution)/shard_map/dot_general | solution.py:101
  131.7 4.2 %fusion.10 = (f32[384]{0:T(512)S(1)}, f32[384,2048]{1,0:T(8,128)S(1)}) fusion(bf16[2,384,2048]{2,1,0:T(8,128)(2,1)} %all-gather.3.cloned.1.call-done, f32[2048]{0:T(1024)S(1)} %bitcast.272, f32[384,2048]{1,0:T(8,128)} %fusion.22, bf16[1,2048,512]{2,1,0:T(8,128)(2,1)S(1)} %copy-done, f32[384,512]{1,0:T(8,128)} %fusion.29, f32[384,512]{1,0:T(8,128)} %fusion.24), kind=kOutput, calls=%fused_computation.17 | convolution fusion | flops 810417792 | bytes 11544064 | tf_op jit(solution)/shard_map/dot_general | solution.py:104
  136.5 1.2 copy.45
  137.8 5.0 %all-to-all-start.3 = ((bf16[8,384,256]{2,1,0:T(8,128)(2,1)}), bf16[8,384,256]{2,1,0:T(8,128)(2,1)}, u32[]{:S(2)}, u32[]{:S(2)}) async-start(bf16[8,384,256]{2,1,0:T(8,128)(2,1)} %bitcast.250), calls=%async_computation.3 | async-start | bytes 3145728 | tf_op jit(solution)/shard_map/all_to_all | solution.py:18
  143.3 1.9 sort.32
  145.2 1.2 compare_select_fusion.1
  146.4 1.2 compare_and_fusion.1
  147.5 13.8 %all-to-all-done.3 = bf16[8,384,256]{2,1,0:T(8,128)(2,1)} async-done(((bf16[8,384,256]{2,1,0:T(8,128)(2,1)}), bf16[8,384,256]{2,1,0:T(8,128)(2,1)}, u32[]{:S(2)}, u32[]{:S(2)}) %all-to-all-start.3) | async-done | bytes 1572896 | tf_op jit(solution)/shard_map/all_to_all | solution.py:18
  161.3 1.7 convert_reduce_fusion.1
  163.7 4.4 %all-to-all-start.4 = ((bf16[1,16,24,256]{3,2,0,1:T(8,128)(2,1)}), bf16[1,16,24,256]{3,2,0,1:T(8,128)(2,1)S(1)}, u32[]{:S(2)}, u32[]{:S(2)}) async-start(bf16[1,16,24,256]{3,2,0,1:T(8,128)(2,1)} %add_convert_fusion), calls=%async_computation.4 | async-start | bytes 393216 | tf_op jit(solution)/shard_map/all_to_all | solution.py:118
  168.8 5.7 %all-to-all-done.4 = bf16[1,16,24,256]{3,2,0,1:T(8,128)(2,1)S(1)} async-done(((bf16[1,16,24,256]{3,2,0,1:T(8,128)(2,1)}), bf16[1,16,24,256]{3,2,0,1:T(8,128)(2,1)S(1)}, u32[]{:S(2)}, u32[]{:S(2)}) %all-to-all-start.4) | async-done | bytes 196640 | tf_op jit(solution)/shard_map/all_to_all | solution.py:118
  174.4 1.2 gather_fusion.1
  175.7 1.0 fusion.94
  176.7 15.7 %all_to_all.36 = bf16[1,16,24,256]{3,2,0,1:T(8,128)(2,1)} all-to-all(bf16[1,16,24,256]{3,2,0,1:T(8,128)(2,1)S(1)} %fusion.94), channel_id=1, replica_groups=mesh['client'=16,'tensor'=8,'sdata'=2] {'client'}, dimensions={1} | all-to-all | bytes 393216 | tf_op jit(solution)/shard_map/all_to_all | solution.py:114
  192.5 23.7 %all-gather.5.cloned.1.call-done = bf16[1,384,2048]{2,1,0:T(8,128)(2,1)} async-done(((bf16[1,384,256]{2,1,0:T(8,128)(2,1)}), bf16[1,384,2048]{2,1,0:T(8,128)(2,1)}) %all-gather.5.cloned.1.call-update) | async-done | bytes 1572880 | tf_op jit(solution)/shard_map/all_gather | solution.py:140
  216.2 2.3 fusion.57
  218.5 1.7 fusion.21
  220.3 1.1 broadcast_multiply_fusion
  221.4 1.2 fusion.68
  222.7 4.1 %convolution_convert_fusion.3 = bf16[2048,64]{0,1:T(8,128)(2,1)} fusion(bf16[64,4,384]{2,0,1:T(8,128)(2,1)S(1)} %bitcast.269, f32[4,384]{1,0:T(4,128)S(1)} %copy-done.27, f32[4,384]{1,0:T(4,128)S(1)} %get-tuple-element.27, f32[384,384,4]{1,0,2:T(8,128)} %copy-done.1, pred[384,384]{0,1:T(8,128)(4,1)S(1)} %copy-done.9, bf16[384,2048]{1,0:T(8,128)(2,1)} %param.12, ...), kind=kOutput, calls=%fused_computation.41 | convolution fusion | flops 182411264 | bytes 4560384 | tf_op jit(solution)/shard_map/transpose(jvp())/dot_general | solution.py:64
  226.9 3.4 %convolution_convert_fusion.2 = bf16[2048,256]{1,0:T(8,128)(2,1)} fusion(bf16[384,256]{0,1:T(8,128)(2,1)S(1)} %bitcast.267, bf16[384,2048]{1,0:T(8,128)(2,1)} %param.12, f32[2048]{0:T(1024)S(1)} %bitcast.277, f32[384]{0:T(512)S(1)} %copy-done.34), kind=kOutput, calls=%fused_computation.28 | convolution fusion | flops 405798912 | bytes 2827776 | tf_op jit(solution)/shard_map/transpose(jvp())/dot_general | solution.py:51
  231.3 1.2 copy.40
  232.5 2.2 convolution_convert_fusion.1
  234.8 1.3 pad_maximum_fusion
  236.0 72.6 %all_to_all.37 = bf16[32,64,640]{2,1,0:T(8,128)(2,1)S(1)} all-to-all(bf16[32,64,640]{2,1,0:T(8,128)(2,1)S(1)} %pad_maximum_fusion), channel_id=1, replica_groups=mesh['client'=16,'tensor'=8,'sdata'=2] {'client','sdata'}, dimensions={0} | all-to-all | bytes 5242880 | tf_op jit(solution)/shard_map/all_to_all | solution.py:18
  (120 shorter events, 13.6 us)
Async XLA Ops:
  7.2 118.2 %copy-start = (bf16[1,2048,512]{2,1,0:T(8,128)(2,1)S(1)}, bf16[1,2048,512]{2,1,0:T(8,128)(2,1)}, u32[]{:S(2)}) copy-start(bf16[1,2048,512]{2,1,0:T(8,128)(2,1)} %param.20) | copy-start | bytes 6291460
  7.3 12.5 %copy-start.8 = (pred[384,384]{0,1:T(8,128)(4,1)}, pred[384,384]{0,1:T(8,128)(4,1)S(1)}, u32[]{:S(2)}) copy-start(pred[384,384]{0,1:T(8,128)(4,1)S(1)} %iota_compare_fusion) | copy-start | bytes 442372
  8.1 8.2 %copy-start.31 = (f32[1,2048]{1,0:T(1,128)}, f32[1,2048]{1,0:T(1,128)S(1)}, u32[]{:S(2)}) copy-start(f32[1,2048]{1,0:T(1,128)S(1)} %mul.298) | copy-start | bytes 24580
  8.1 4.0 %copy-start.10 = (bf16[1,2048,256]{2,1,0:T(8,128)(2,1)S(1)}, bf16[1,2048,256]{2,1,0:T(8,128)(2,1)}, u32[]{:S(2)}) copy-start(bf16[1,2048,256]{2,1,0:T(8,128)(2,1)} %param.14) | copy-start | bytes 3145732
  10.0 6.2 %copy-start.33 = (f32[384]{0:T(512)}, f32[384]{0:T(512)S(1)}, u32[]{:S(2)}) copy-start(f32[384]{0:T(512)S(1)} %add_rsqrt_fusion.1) | copy-start | bytes 4612
  13.6 2.7 copy-start.6
  13.6 2.7 copy-start.36
  17.0 2.8 copy-start.38
  17.2 2.0 copy-start.18
  17.3 2.0 copy-start.22
  17.3 0.7 copy-start.12
  17.3 1.9 copy-start.20
  17.3 1.9 copy-start.24
  17.9 0.7 copy-start.14
  19.2 1.5 copy-start.1
  19.8 0.9 copy-start.26
  19.8 1.5 copy-start.5
  20.7 2.4 copy-start.16
  23.1 24.9 %all-to-all-start = ((bf16[8,384,256]{2,1,0:T(8,128)(2,1)}), bf16[8,384,256]{2,1,0:T(8,128)(2,1)}, u32[]{:S(2)}, u32[]{:S(2)}) async-start(bf16[8,384,256]{2,1,0:T(8,128)(2,1)} %bitcast.249), calls=%async_computation | async-start | bytes 3145728 | tf_op jit(solution)/shard_map/all_to_all | solution.py:18
  29.5 30.0 %copy-start.37 = (s32[16]{0:T(128)S(1)}, s32[16]{0:T(128)}, u32[]{:S(2)}) copy-start(s32[16]{0:T(128)} %param.23) | copy-start | bytes 196
  51.5 20.7 %all-to-all-start.1 = ((bf16[2,16,24,256]{3,2,0,1:T(8,128)(2,1)}), bf16[2,16,24,256]{3,2,0,1:T(8,128)(2,1)S(1)}, u32[]{:S(2)}, u32[]{:S(2)}) async-start(bf16[2,16,24,256]{3,2,0,1:T(8,128)(2,1)} %pad_maximum_fusion.1), calls=%async_computation.1 | async-start | bytes 786432 | tf_op jit(solution)/shard_map/all_to_all | solution.py:114
  59.5 57.4 %all-gather.3.cloned.1.call-start = ((), (), s32[]{:S(2)}) async-start(), calls=%async_computation.7 | async-start | bytes 3538944 | tf_op jit(solution)/shard_map/all_gather | solution.py:140
  119.3 4.2 %copy-start.29 = (f32[384]{0:T(512)}, f32[384]{0:T(512)S(1)}, u32[]{:S(2)}) copy-start(f32[384]{0:T(512)S(1)} %get-tuple-element.26) | copy-start | bytes 4612
  119.3 4.2 %copy-start.3 = (bf16[2,384,2048]{2,1,0:T(8,128)(2,1)S(1)}, bf16[2,384,2048]{2,1,0:T(8,128)(2,1)}, u32[]{:S(2)}) copy-start(bf16[2,384,2048]{2,1,0:T(8,128)(2,1)} %all-gather.3.cloned.1.call-done) | copy-start | bytes 9437188
  119.3 4.2 %copy-start.35 = (bf16[1,2048,512]{2,1,0:T(8,128)(2,1)S(1)}, bf16[1,2048,512]{2,1,0:T(8,128)(2,1)}, u32[]{:S(2)}) copy-start(bf16[1,2048,512]{2,1,0:T(8,128)(2,1)} %param.19) | copy-start | bytes 6291460
  131.6 4.2 %copy-start.4 = (bf16[2,384,2048]{2,1,0:T(8,128)(2,1)S(1)}, bf16[2,384,2048]{2,1,0:T(8,128)(2,1)}, u32[]{:S(2)}) copy-start(bf16[2,384,2048]{2,1,0:T(8,128)(2,1)} %all-gather.3.cloned.1.call-done) | copy-start | bytes 9437188
  131.6 4.2 %copy-start.28 = (f32[384]{0:T(512)S(1)}, f32[384]{0:T(512)}, u32[]{:S(2)}) copy-start(f32[384]{0:T(512)} %get-tuple-element.25) | copy-start | bytes 4612
  131.7 4.2 %copy-start.30 = (f32[384]{0:T(512)S(1)}, f32[384]{0:T(512)}, u32[]{:S(2)}) copy-start(f32[384]{0:T(512)} %copy-done.29) | copy-start | bytes 4612
  137.8 23.5 %all-to-all-start.3 = ((bf16[8,384,256]{2,1,0:T(8,128)(2,1)}), bf16[8,384,256]{2,1,0:T(8,128)(2,1)}, u32[]{:S(2)}, u32[]{:S(2)}) async-start(bf16[8,384,256]{2,1,0:T(8,128)(2,1)} %bitcast.250), calls=%async_computation.3 | async-start | bytes 3145728 | tf_op jit(solution)/shard_map/all_to_all | solution.py:18
  142.8 49.7 %copy-start.27 = (f32[4,384]{1,0:T(4,128)S(1)}, f32[4,384]{1,0:T(4,128)}, u32[]{:S(2)}) copy-start(f32[4,384]{1,0:T(4,128)} %copy-done.26) | copy-start | bytes 18436
  163.7 54.8 %copy-start.9 = (pred[384,384]{0,1:T(8,128)(4,1)S(1)}, pred[384,384]{0,1:T(8,128)(4,1)}, u32[]{:S(2)}) copy-start(pred[384,384]{0,1:T(8,128)(4,1)} %copy-done.8) | copy-start | bytes 442372
  163.7 10.7 %all-to-all-start.4 = ((bf16[1,16,24,256]{3,2,0,1:T(8,128)(2,1)}), bf16[1,16,24,256]{3,2,0,1:T(8,128)(2,1)S(1)}, u32[]{:S(2)}, u32[]{:S(2)}) async-start(bf16[1,16,24,256]{3,2,0,1:T(8,128)(2,1)} %add_convert_fusion), calls=%async_computation.4 | async-start | bytes 393216 | tf_op jit(solution)/shard_map/all_to_all | solution.py:118
  168.1 48.0 %all-gather.5.cloned.1.call-start = ((), (), s32[]{:S(2)}) async-start(), calls=%async_computation.8 | async-start | bytes 1769472 | tf_op jit(solution)/shard_map/all_gather | solution.py:140
  216.2 2.3 copy-start.2
  218.5 1.8 copy-start.21
  218.5 1.8 copy-start.25
  220.3 1.1 copy-start.15
  221.4 1.2 copy-start.32
  221.4 1.2 copy-start.34
  222.7 4.2 %copy-start.13 = (f32[384,64]{0,1:T(8,128)S(1)}, f32[384,64]{0,1:T(8,128)}, u32[]{:S(2)}) copy-start(f32[384,64]{0,1:T(8,128)} %copy-done.12) | copy-start | bytes 294916
  226.8 3.5 %copy-start.19 = (f32[384,32]{0,1:T(8,128)S(1)}, f32[384,32]{0,1:T(8,128)}, u32[]{:S(2)}) copy-start(f32[384,32]{0,1:T(8,128)} %copy-done.18) | copy-start | bytes 147460
  226.9 3.5 %copy-start.7 = (bf16[384,2048]{1,0:T(8,128)(2,1)S(1)}, bf16[384,2048]{1,0:T(8,128)(2,1)}, u32[]{:S(2)}) copy-start(bf16[384,2048]{1,0:T(8,128)(2,1)} %param.12) | copy-start | bytes 4718596
  226.9 3.5 %copy-start.23 = (f32[384,32]{0,1:T(8,128)S(1)}, f32[384,32]{0,1:T(8,128)}, u32[]{:S(2)}) copy-start(f32[384,32]{0,1:T(8,128)} %copy-done.22) | copy-start | bytes 147460
  230.3 2.2 copy-start.17
  232.5 2.3 copy-start.11
Sparse Core Ops, SparseCore 0:
  86.9 29.9 all-gather.2
  192.6 23.5 all-gather.4
where the time goes:
time: 318 us; the launch traced here: 317 us
  waiting for transfers between devices  100 us (31%)
  blocking collectives  99.6 us (31%)
  matrix products  40.7 us (13%)
  starting transfers between devices  23.9 us (8%)
  other arithmetic  23.6 us (7%)
  between operations  14.7 us (5%)
  local copies, waits for them, and re-layouts  14.5 us (5%)
    all_to_all x1, blocking collectives, sum_at_owner(): lax.all_to_all(cut_along(value, dim, length), axis, 0, 0, tiled=True)  72.6 us
    all_gather x2, waiting for transfers between devices, widen_rows(): return lax.all_gather(stacked, 'tensor', axis=2, tiled=True)  53.1 us
    all_to_all x2, waiting for transfers between devices, sum_at_owner(): lax.all_to_all(cut_along(value, dim, length), axis, 0, 0, tiled=True)  31.3 us
    all_to_all x1, blocking collectives, over_clients(): lax.all_to_all(pieces, 'client', split_axis=1, concat_axis=1, tiled=True)  15.7 us
    all_to_all x2, starting transfers between devices, sum_at_owner(): lax.all_to_all(cut_along(value, dim, length), axis, 0, 0, tiled=True)  11.4 us
    all_to_all x1, blocking collectives, over_groups(): lax.all_to_all(pieces, 'sdata', split_axis=1, concat_axis=1, tiled=True)  11.3 us
    all_to_all x1, waiting for transfers between devices, over_clients(): lax.all_to_all(pieces, 'client', split_axis=1, concat_axis=1, tiled=True)  10.1 us
    all_to_all x1, starting transfers between devices, over_clients(): lax.all_to_all(pieces, 'client', split_axis=1, concat_axis=1, tiled=True)  8.01 us
  transfers between devices with their start and end apart: 6, of which 6 were waited for; matrix products, arithmetic and copies ran while one was open for 3% of the time, Pallas kernels for 0%

commit v1 on v0

--- a/solution.py
+++ b/solution.py
@@ -1,3 +1,4 @@
+import functools
 from functools import partial
 import math
 import jax
@@ -6,6 +7,25 @@
 from jax.sharding import PartitionSpec as P
 
 HEAD_DIM = 64
+
+
+def lift_bars(view, mesh_name, dim_no):
+    many = jax.lax.axis_size(mesh_name)
+    panels = list(map(lambda b: (b, (b + 1) % many), range(many)))
+    cards = list(map(lambda b: (b, (b - 1) % many), range(many)))
+    heard, lower = ([view], [view])
+    for _ in range(many // 2):
+        heard.append(jax.lax.ppermute(heard[-1], perm=panels, axis_name=mesh_name))
+    for _ in range((many - 1) // 2):
+        lower.append(jax.lax.ppermute(lower[-1], axis_name=mesh_name, perm=cards))
+    return jnp.roll(
+        jnp.concatenate([*heard[::-1], *lower[1:]], axis=dim_no),
+        (jax.lax.axis_index(mesh_name) - many // 2) * view.shape[dim_no],
+        axis=dim_no,
+    )
+
+
+_hold_yards = functools.partial(lift_bars, mesh_name="tensor", dim_no=2)
 
 
 def cut_along(value, dim, length):
@@ -137,7 +157,7 @@
 
 
 def widen_rows(stacked):
-    return lax.all_gather(stacked, "tensor", axis=2, tiled=True)
+    return _hold_yards(stacked)
 
 
 def local(

time: 318 us -> 312 us (0.981)
  starting transfers between devices: 23.9 us -> 41.1 us
  waiting for transfers between devices: 100 us -> 84.1 us
  local copies, waits for them, and re-layouts: 14.5 us -> 27.8 us
  between operations: 14.7 us -> 1.65 us
  blocking collectives: 99.6 us -> 92.2 us
  matrix products: 40.7 us -> 36.9 us
    all_gather x2 -> x0, waiting for transfers between devices: 53.1 us -> none  [widen_rows(): return lax.all_gather(stacked, 'tensor', axis=2, tiled=True)]
    ppermute x0 -> x14, waiting for transfers between devices: none -> 37.6 us  [the longest x8 37.5 us: lift_bars(): heard.append(jax.lax.ppermute(heard[-1], perm=panels, axis_name=mesh_name))]
    unnamed x79 -> x125, local copies, waits for them, and re-layouts: 3.43 us -> 16.5 us
    ppermute x0 -> x14, starting transfers between devices: none -> 11.3 us  [the longest x6 11 us: lift_bars(): lower.append(jax.lax.ppermute(lower[-1], axis_name=mesh_name, perm=cards))]
    all_to_all x2, starting transfers between devices: 11.4 us -> 18.3 us  [sum_at_owner(): lax.all_to_all(cut_along(value, dim, length), axis, 0, 0, tiled=True)]
    all_to_all x1, blocking collectives: 72.6 us -> 67.9 us  [sum_at_owner(): lax.all_to_all(cut_along(value, dim, length), axis, 0, 0, tiled=True)]
  transfers between devices with their start and end apart: 6 -> 18, of which waited for: 6 -> 13; matrix products, arithmetic and copies ran while one was open for 3% -> 5% of each run, Pallas kernels for 0% -> 0%
where the time goes in v1:
time: 312 us; the launch traced here: 309 us
  blocking collectives  92.2 us (30%)
  waiting for transfers between devices  84.1 us (27%)
  starting transfers between devices  41.1 us (13%)
  matrix products  36.9 us (12%)
  local copies, waits for them, and re-layouts  27.8 us (9%)
  other arithmetic  25.6 us (8%)
    all_to_all x1, blocking collectives, sum_at_owner(): lax.all_to_all(cut_along(value, dim, length), axis, 0, 0, tiled=True)  67.9 us
    ppermute x8, waiting for transfers between devices, lift_bars(): heard.append(jax.lax.ppermute(heard[-1], perm=panels, axis_name=mesh_name))  37.5 us
    all_to_all x2, waiting for transfers between devices, sum_at_owner(): lax.all_to_all(cut_along(value, dim, length), axis, 0, 0, tiled=True)  31.2 us
    all_to_all x2, starting transfers between devices, sum_at_owner(): lax.all_to_all(cut_along(value, dim, length), axis, 0, 0, tiled=True)  18.3 us
    unnamed x125, local copies, waits for them, and re-layouts  16.5 us
    all_to_all x1, blocking collectives, over_clients(): lax.all_to_all(pieces, 'client', split_axis=1, concat_axis=1, tiled=True)  13 us
    all_to_all x1, blocking collectives, over_groups(): lax.all_to_all(pieces, 'sdata', split_axis=1, concat_axis=1, tiled=True)  11.4 us
    ppermute x6, starting transfers between devices, lift_bars(): lower.append(jax.lax.ppermute(lower[-1], axis_name=mesh_name, perm=cards))  11 us
  transfers between devices with their start and end apart: 18, of which 13 were waited for; matrix products, arithmetic and copies ran while one was open for 5% of the time, Pallas kernels for 0%

profile of v1, /device:TPU:4, one launch (start us, length us, event | category | flops | bytes accessed | tf_op | source)
XLA Modules:
  0.0 309.3 jit_solution(15963666010880031246)
XLA Ops:
  1.7 1.8 fusion.3
  3.5 2.1 fusion.93
  5.6 1.4 copy.27
  7.1 2.6 fusion.36
  16.0 6.4 %all-to-all-start = ((bf16[8,384,256]{2,1,0:T(8,128)(2,1)}), bf16[8,384,256]{2,1,0:T(8,128)(2,1)}, u32[]{:S(2)}, u32[]{:S(2)}) async-start(bf16[8,384,256]{2,1,0:T(8,128)(2,1)} %bitcast.249), calls=%async_computation | async-start | bytes 3145728 | tf_op jit(solution)/shard_map/all_to_all | solution.py:38
  23.3 17.5 %all-to-all-done = bf16[8,384,256]{2,1,0:T(8,128)(2,1)} async-done(((bf16[8,384,256]{2,1,0:T(8,128)(2,1)}), bf16[8,384,256]{2,1,0:T(8,128)(2,1)}, u32[]{:S(2)}, u32[]{:S(2)}) %all-to-all-start) | async-done | bytes 1572896 | tf_op jit(solution)/shard_map/all_to_all | solution.py:38
  40.9 1.7 convert_reduce_fusion.2
  44.3 8.0 %all-to-all-start.1 = ((bf16[2,16,24,256]{3,2,0,1:T(8,128)(2,1)}), bf16[2,16,24,256]{3,2,0,1:T(8,128)(2,1)S(1)}, u32[]{:S(2)}, u32[]{:S(2)}) async-start(bf16[2,16,24,256]{3,2,0,1:T(8,128)(2,1)} %pad_maximum_fusion.1), calls=%async_computation.1 | async-start | bytes 786432 | tf_op jit(solution)/shard_map/all_to_all | solution.py:134
  52.3 1.3 sort.31
  54.9 10.1 %all-to-all-done.1 = bf16[2,16,24,256]{3,2,0,1:T(8,128)(2,1)S(1)} async-done(((bf16[2,16,24,256]{3,2,0,1:T(8,128)(2,1)}), bf16[2,16,24,256]{3,2,0,1:T(8,128)(2,1)S(1)}, u32[]{:S(2)}, u32[]{:S(2)}) %all-to-all-start.1) | async-done | bytes 393248 | tf_op jit(solution)/shard_map/all_to_all | solution.py:134
  65.8 1.6 gather_fusion
  67.5 11.4 %all_to_all.35 = bf16[2,16,24,256]{3,2,0,1:T(8,128)(2,1)S(1)} all-to-all(bf16[2,16,24,256]{3,2,0,1:T(8,128)(2,1)S(1)} %select_bitcast_fusion), channel_id=1, replica_groups=mesh['client'=16,'tensor'=8,'sdata'=2] {'sdata'}, dimensions={1} | all-to-all | bytes 786432 | tf_op jit(solution)/shard_map/all_to_all | solution.py:138
  78.9 7.2 %collective-permute-done = bf16[2,384,256]{2,1,0:T(8,128)(2,1)S(1)} collective-permute-done((bf16[2,384,256]{2,1,0:T(8,128)(2,1)S(1)}, bf16[2,384,256]{2,1,0:T(8,128)(2,1)S(1)}, u32[]{:S(2)}, u32[]{:S(2)}) %collective-permute-start) | collective-permute-done | bytes 393248 | tf_op jit(solution)/shard_map/ppermute | solution.py:18
  86.1 1.7 collective-permute-start.4
  87.8 5.5 %collective-permute-done.1 = bf16[2,384,256]{2,1,0:T(8,128)(2,1)S(1)} collective-permute-done((bf16[2,384,256]{2,1,0:T(8,128)(2,1)S(1)}, bf16[2,384,256]{2,1,0:T(8,128)(2,1)S(1)}, u32[]{:S(2)}, u32[]{:S(2)}) %collective-permute-start.1) | collective-permute-done | bytes 393248 | tf_op jit(solution)/shard_map/ppermute | solution.py:18
  93.3 1.8 collective-permute-start.5
  95.1 5.5 %collective-permute-done.2 = bf16[2,384,256]{2,1,0:T(8,128)(2,1)} collective-permute-done((bf16[2,384,256]{2,1,0:T(8,128)(2,1)S(1)}, bf16[2,384,256]{2,1,0:T(8,128)(2,1)}, u32[]{:S(2)}, u32[]{:S(2)}) %collective-permute-start.2) | collective-permute-done | bytes 393248 | tf_op jit(solution)/shard_map/ppermute | solution.py:18
  101.3 1.8 collective-permute-start.6
  103.1 5.0 %collective-permute-done.3 = bf16[2,384,256]{2,1,0:T(8,128)(2,1)} collective-permute-done((bf16[2,384,256]{2,1,0:T(8,128)(2,1)}, bf16[2,384,256]{2,1,0:T(8,128)(2,1)}, u32[]{:S(2)}, u32[]{:S(2)}) %collective-permute-start.3) | collective-permute-done | bytes 393248 | tf_op jit(solution)/shard_map/ppermute | solution.py:18
  119.7 1.9 fusion.29
  122.8 1.9 fusion.24
  124.7 6.3 %fusion.22 = f32[384,2048]{1,0:T(8,128)} fusion(bf16[1,2048,512]{2,1,0:T(8,128)(2,1)} %param.19, f32[384,512]{1,0:T(8,128)} %fusion.29, bf16[1,2048,512]{2,1,0:T(8,128)(2,1)S(1)} %copy-done, f32[384,512]{1,0:T(8,128)} %fusion.24, f32[2048]{0:T(1024)S(1)} %bitcast.277, f32[384]{0:T(512)S(1)} %get-tuple-element.26, bf16[2,384,4096]{2,1,0:T(8,128)(2,1)} %copy-done.4, ...), kind=kOutput, calls=%fused_computation.43 | convolution fusion | flops 1615724544 | bytes 10495492 | tf_op jit(solution)/shard_map/dot_general | solution.py:121
  131.0 4.1 %fusion.10 = (f32[384]{0:T(512)S(1)}, f32[384,2048]{1,0:T(8,128)S(1)}) fusion(bf16[2,384,4096]{2,1,0:T(8,128)(2,1)} %copy-done.4, s32[]{:T(128)S(6)} %select_n.62, f32[2048]{0:T(1024)S(1)} %bitcast.278, f32[384,2048]{1,0:T(8,128)} %fusion.22, bf16[1,2048,512]{2,1,0:T(8,128)(2,1)S(1)} %copy-done, f32[384,512]{1,0:T(8,128)} %fusion.29, f32[384,512]{1,0:T(8,128)} %fusion.24), kind=kOutput, calls=%fused_computation.17 | convolution fusion | flops 810417792 | bytes 11544068 | tf_op jit(solution)/shard_map/dot_general | solution.py:124
  135.1 2.0 fusion.9
  138.4 11.9 %all-to-all-start.3 = ((bf16[8,384,256]{2,1,0:T(8,128)(2,1)}), bf16[8,384,256]{2,1,0:T(8,128)(2,1)}, u32[]{:S(2)}, u32[]{:S(2)}) async-start(bf16[8,384,256]{2,1,0:T(8,128)(2,1)} %bitcast.250), calls=%async_computation.3 | async-start | bytes 3145728 | tf_op jit(solution)/shard_map/all_to_all | solution.py:38
  150.9 1.9 sort.32
  155.2 13.7 %all-to-all-done.3 = bf16[8,384,256]{2,1,0:T(8,128)(2,1)} async-done(((bf16[8,384,256]{2,1,0:T(8,128)(2,1)}), bf16[8,384,256]{2,1,0:T(8,128)(2,1)}, u32[]{:S(2)}, u32[]{:S(2)}) %all-to-all-start.3) | async-done | bytes 1572896 | tf_op jit(solution)/shard_map/all_to_all | solution.py:38
  168.9 1.7 convert_reduce_fusion.1
  171.3 3.4 %all-to-all-start.4 = ((bf16[1,16,24,256]{3,2,0,1:T(8,128)(2,1)}), bf16[1,16,24,256]{3,2,0,1:T(8,128)(2,1)S(1)}, u32[]{:S(2)}, u32[]{:S(2)}) async-start(bf16[1,16,24,256]{3,2,0,1:T(8,128)(2,1)} %add_convert_fusion), calls=%async_computation.4 | async-start | bytes 393216 | tf_op jit(solution)/shard_map/all_to_all | solution.py:138
  175.9 5.1 %all-to-all-done.4 = bf16[1,16,24,256]{3,2,0,1:T(8,128)(2,1)S(1)} async-done(((bf16[1,16,24,256]{3,2,0,1:T(8,128)(2,1)}), bf16[1,16,24,256]{3,2,0,1:T(8,128)(2,1)S(1)}, u32[]{:S(2)}, u32[]{:S(2)}) %all-to-all-start.4) | async-done | bytes 196640 | tf_op jit(solution)/shard_map/all_to_all | solution.py:138
  182.4 13.0 %all_to_all.36 = bf16[1,16,24,256]{3,2,0,1:T(8,128)(2,1)S(1)} all-to-all(bf16[1,16,24,256]{3,2,0,1:T(8,128)(2,1)S(1)} %fusion.96), channel_id=1, replica_groups=mesh['client'=16,'tensor'=8,'sdata'=2] {'client'}, dimensions={1} | all-to-all | bytes 393216 | tf_op jit(solution)/shard_map/all_to_all | solution.py:134
  195.4 5.1 %collective-permute-done.7 = bf16[1,384,256]{2,1,0:T(8,128)(2,1)S(1)} collective-permute-done((bf16[1,384,256]{2,1,0:T(8,128)(2,1)S(1)}, bf16[1,384,256]{2,1,0:T(8,128)(2,1)S(1)}, u32[]{:S(2)}, u32[]{:S(2)}) %collective-permute-start.7) | collective-permute-done | bytes 196640 | tf_op jit(solution)/shard_map/ppermute | solution.py:18
  200.6 1.6 collective-permute-start.11
  202.2 3.3 %collective-permute-done.8 = bf16[1,384,256]{2,1,0:T(8,128)(2,1)S(1)} collective-permute-done((bf16[1,384,256]{2,1,0:T(8,128)(2,1)S(1)}, bf16[1,384,256]{2,1,0:T(8,128)(2,1)S(1)}, u32[]{:S(2)}, u32[]{:S(2)}) %collective-permute-start.8) | collective-permute-done | bytes 196640 | tf_op jit(solution)/shard_map/ppermute | solution.py:18
  205.7 1.9 collective-permute-start.12
  207.6 3.1 collective-permute-done.9
  210.8 2.1 collective-permute-start.13
  212.9 2.9 collective-permute-done.10
  217.1 1.3 copy-done.2
  219.4 2.0 broadcast_multiply_fusion
  221.5 1.8 fusion.70
  223.3 4.2 %convolution_convert_fusion.3 = bf16[2048,64]{0,1:T(8,128)(2,1)} fusion(bf16[64,4,384]{2,0,1:T(8,128)(2,1)} %bitcast.274, f32[4,384]{1,0:T(4,128)S(1)} %copy-done.36, f32[4,384]{1,0:T(4,128)S(1)} %get-tuple-element.27, f32[384,384,4]{1,0,2:T(8,128)} %copy-done.1, pred[384,384]{0,1:T(8,128)(4,1)S(1)} %copy-done.15, bf16[384,2048]{1,0:T(8,128)(2,1)} %param.12, ...), kind=kOutput, calls=%fused_computation.41 | convolution fusion | flops 182411264 | bytes 4560384 | tf_op jit(solution)/shard_map/transpose(jvp())/dot_general | solution.py:84
  227.5 2.3 convolution_convert_fusion.1
  231.0 1.9 convolution_convert_fusion.2
  233.0 1.3 convolution_convert_fusion.4
  234.3 2.0 copy.39
  237.3 2.4 pad_maximum_fusion
  239.7 67.9 %all_to_all.37 = bf16[32,64,640]{2,1,0:T(8,128)(2,1)S(1)} all-to-all(bf16[32,64,640]{2,1,0:T(8,128)(2,1)S(1)} %pad_maximum_fusion), channel_id=1, replica_groups=mesh['client'=16,'tensor'=8,'sdata'=2] {'client','sdata'}, dimensions={0} | all-to-all | bytes 5242880 | tf_op jit(solution)/shard_map/all_to_all | solution.py:38
  (190 shorter events, 39.3 us)
Async XLA Ops:
  0.6 124.1 %copy-start = (bf16[1,2048,512]{2,1,0:T(8,128)(2,1)S(1)}, bf16[1,2048,512]{2,1,0:T(8,128)(2,1)}, u32[]{:S(2)}) copy-start(bf16[1,2048,512]{2,1,0:T(8,128)(2,1)} %param.20) | copy-start | bytes 6291460
  0.6 5.0 %copy-start.16 = (bf16[1,2048,256]{2,1,0:T(8,128)(2,1)S(1)}, bf16[1,2048,256]{2,1,0:T(8,128)(2,1)}, u32[]{:S(2)}) copy-start(bf16[1,2048,256]{2,1,0:T(8,128)(2,1)} %param.14) | copy-start | bytes 3145732
  0.7 11.9 %copy-start.14 = (pred[384,384]{0,1:T(8,128)(4,1)}, pred[384,384]{0,1:T(8,128)(4,1)S(1)}, u32[]{:S(2)}) copy-start(pred[384,384]{0,1:T(8,128)(4,1)S(1)} %iota_compare_fusion) | copy-start | bytes 442372
  1.7 8.1 %copy-start.37 = (f32[1,2048]{1,0:T(1,128)}, f32[1,2048]{1,0:T(1,128)S(1)}, u32[]{:S(2)}) copy-start(f32[1,2048]{1,0:T(1,128)S(1)} %mul.303) | copy-start | bytes 24580
  3.5 6.3 %copy-start.39 = (f32[384]{0:T(512)}, f32[384]{0:T(512)S(1)}, u32[]{:S(2)}) copy-start(f32[384]{0:T(512)S(1)} %add_rsqrt_fusion.1) | copy-start | bytes 4612
  7.1 2.7 copy-start.8
  7.1 2.7 copy-start.43
  16.0 24.9 %all-to-all-start = ((bf16[8,384,256]{2,1,0:T(8,128)(2,1)}), bf16[8,384,256]{2,1,0:T(8,128)(2,1)}, u32[]{:S(2)}, u32[]{:S(2)}) async-start(bf16[8,384,256]{2,1,0:T(8,128)(2,1)} %bitcast.249), calls=%async_computation | async-start | bytes 3145728 | tf_op jit(solution)/shard_map/all_to_all | solution.py:38
  22.4 30.0 %copy-start.44 = (s32[16]{0:T(128)S(1)}, s32[16]{0:T(128)}, u32[]{:S(2)}) copy-start(s32[16]{0:T(128)} %param.23) | copy-start | bytes 196
  44.3 20.7 %all-to-all-start.1 = ((bf16[2,16,24,256]{3,2,0,1:T(8,128)(2,1)}), bf16[2,16,24,256]{3,2,0,1:T(8,128)(2,1)S(1)}, u32[]{:S(2)}, u32[]{:S(2)}) async-start(bf16[2,16,24,256]{3,2,0,1:T(8,128)(2,1)} %pad_maximum_fusion.1), calls=%async_computation.1 | async-start | bytes 786432 | tf_op jit(solution)/shard_map/all_to_all | solution.py:134
  78.8 14.5 %copy-start.6 = (bf16[2,16,24,256]{3,2,0,1:T(8,128)(2,1)}, bf16[2,16,24,256]{3,2,0,1:T(8,128)(2,1)S(1)}, u32[]{:S(2)}) copy-start(bf16[2,16,24,256]{3,2,0,1:T(8,128)(2,1)S(1)} %all_to_all.35) | copy-start | bytes 1179652
  78.8 7.2 %collective-permute-start = (bf16[2,384,256]{2,1,0:T(8,128)(2,1)S(1)}, bf16[2,384,256]{2,1,0:T(8,128)(2,1)S(1)}, u32[]{:S(2)}, u32[]{:S(2)}) collective-permute-start(bf16[2,384,256]{2,1,0:T(8,128)(2,1)S(1)} %bitcast.254), channel_id=1, source_target_pairs={{0,2},{2,4},{4,6},{6,8},{8,10},{10,12},{12,14},{14,0},{1,3},{3,5},... | collective-permute-start | bytes 1179656 | tf_op jit(solution)/shard_map/ppermute | solution.py:18
  86.1 9.1 %copy-start.10 = (bf16[2,384,256]{2,1,0:T(8,128)(2,1)}, bf16[2,384,256]{2,1,0:T(8,128)(2,1)S(1)}, u32[]{:S(2)}) copy-start(bf16[2,384,256]{2,1,0:T(8,128)(2,1)S(1)} %collective-permute-done) | copy-start | bytes 1179652
  86.1 7.2 %collective-permute-start.1 = (bf16[2,384,256]{2,1,0:T(8,128)(2,1)S(1)}, bf16[2,384,256]{2,1,0:T(8,128)(2,1)S(1)}, u32[]{:S(2)}, u32[]{:S(2)}) collective-permute-start(bf16[2,384,256]{2,1,0:T(8,128)(2,1)S(1)} %collective-permute-done), channel_id=1, source_target_pairs={{0,2},{2,4},{4,6},{6,8},{8,10},{10,12},{12,14},{14,0},{1,3},{3,5},... | collective-permute-start | bytes 1179656 | tf_op jit(solution)/shard_map/ppermute | solution.py:18
  86.1 7.2 %collective-permute-start.4 = (bf16[2,384,256]{2,1,0:T(8,128)(2,1)S(1)}, bf16[2,384,256]{2,1,0:T(8,128)(2,1)}, u32[]{:S(2)}, u32[]{:S(2)}) collective-permute-start(bf16[2,384,256]{2,1,0:T(8,128)(2,1)S(1)} %bitcast.255), channel_id=1, source_target_pairs={{0,14},{2,0},{4,2},{6,4},{8,6},{10,8},{12,10},{14,12},{1,15},{3,1}... | collective-permute-start | bytes 1179656 | tf_op jit(solution)/shard_map/ppermute | solution.py:20
  93.3 7.3 %copy-start.12 = (bf16[2,384,256]{2,1,0:T(8,128)(2,1)}, bf16[2,384,256]{2,1,0:T(8,128)(2,1)S(1)}, u32[]{:S(2)}) copy-start(bf16[2,384,256]{2,1,0:T(8,128)(2,1)S(1)} %collective-permute-done.1) | copy-start | bytes 1179652
  93.3 7.3 %collective-permute-start.2 = (bf16[2,384,256]{2,1,0:T(8,128)(2,1)S(1)}, bf16[2,384,256]{2,1,0:T(8,128)(2,1)}, u32[]{:S(2)}, u32[]{:S(2)}) collective-permute-start(bf16[2,384,256]{2,1,0:T(8,128)(2,1)S(1)} %collective-permute-done.1), channel_id=1, source_target_pairs={{0,2},{2,4},{4,6},{6,8},{8,10},{10,12},{12,14},{14,0},{1,3},{3,5},... | collective-permute-start | bytes 1179656 | tf_op jit(solution)/shard_map/ppermute | solution.py:18
  93.3 8.0 %collective-permute-start.5 = (bf16[2,384,256]{2,1,0:T(8,128)(2,1)}, bf16[2,384,256]{2,1,0:T(8,128)(2,1)}, u32[]{:S(2)}, u32[]{:S(2)}) collective-permute-start(bf16[2,384,256]{2,1,0:T(8,128)(2,1)} %collective-permute-done.4), channel_id=1, source_target_pairs={{0,14},{2,0},{4,2},{6,4},{8,6},{10,8},{12,10},{14,12},{1,15},{3,1}... | collective-permute-start | bytes 1179656 | tf_op jit(solution)/shard_map/ppermute | solution.py:20
  100.6 7.5 %collective-permute-start.3 = (bf16[2,384,256]{2,1,0:T(8,128)(2,1)}, bf16[2,384,256]{2,1,0:T(8,128)(2,1)}, u32[]{:S(2)}, u32[]{:S(2)}) collective-permute-start(bf16[2,384,256]{2,1,0:T(8,128)(2,1)} %collective-permute-done.2), channel_id=1, source_target_pairs={{0,2},{2,4},{4,6},{6,8},{8,10},{10,12},{12,14},{14,0},{1,3},{3,5},... | collective-permute-start | bytes 1179656 | tf_op jit(solution)/shard_map/ppermute | solution.py:18
  101.3 13.3 %collective-permute-start.6 = (bf16[2,384,256]{2,1,0:T(8,128)(2,1)}, bf16[2,384,256]{2,1,0:T(8,128)(2,1)S(1)}, u32[]{:S(2)}, u32[]{:S(2)}) collective-permute-start(bf16[2,384,256]{2,1,0:T(8,128)(2,1)} %collective-permute-done.5), channel_id=1, source_target_pairs={{0,14},{2,0},{4,2},{6,4},{8,6},{10,8},{12,10},{14,12},{1,15},{3,1}... | collective-permute-start | bytes 1179656 | tf_op jit(solution)/shard_map/ppermute | solution.py:20
  110.2 6.6 %copy-start.13 = (bf16[2,384,256]{2,1,0:T(8,128)(2,1)S(1)}, bf16[2,384,256]{2,1,0:T(8,128)(2,1)}, u32[]{:S(2)}) copy-start(bf16[2,384,256]{2,1,0:T(8,128)(2,1)} %copy-done.12) | copy-start | bytes 1179652
  111.3 5.5 %copy-start.11 = (bf16[2,384,256]{2,1,0:T(8,128)(2,1)S(1)}, bf16[2,384,256]{2,1,0:T(8,128)(2,1)}, u32[]{:S(2)}) copy-start(bf16[2,384,256]{2,1,0:T(8,128)(2,1)} %copy-done.10) | copy-start | bytes 1179652
  116.8 2.9 copy-start.41
  119.2 3.1 %copy-start.4 = (bf16[2,384,4096]{2,1,0:T(8,128)(2,1)}, bf16[2,384,4096]{2,1,0:T(8,128)(2,1)S(1)}, u32[]{:S(2)}) copy-start(bf16[2,384,4096]{2,1,0:T(8,128)(2,1)S(1)} %constant_dynamic-update-slice_fusion) | copy-start | bytes 18874372
  119.6 3.2 %copy-start.42 = (bf16[1,2048,512]{2,1,0:T(8,128)(2,1)S(1)}, bf16[1,2048,512]{2,1,0:T(8,128)(2,1)}, u32[]{:S(2)}) copy-start(bf16[1,2048,512]{2,1,0:T(8,128)(2,1)} %param.19) | copy-start | bytes 6291460
  138.4 32.1 %copy-start.7 = (bf16[2,16,24,256]{3,2,0,1:T(8,128)(2,1)S(1)}, bf16[2,16,24,256]{3,2,0,1:T(8,128)(2,1)}, u32[]{:S(2)}) copy-start(bf16[2,16,24,256]{3,2,0,1:T(8,128)(2,1)} %copy-done.6) | copy-start | bytes 1179652
  138.4 72.4 %copy-start.36 = (f32[4,384]{1,0:T(4,128)S(1)}, f32[4,384]{1,0:T(4,128)}, u32[]{:S(2)}) copy-start(f32[4,384]{1,0:T(4,128)} %copy-done.35) | copy-start | bytes 18436
  138.4 30.4 %all-to-all-start.3 = ((bf16[8,384,256]{2,1,0:T(8,128)(2,1)}), bf16[8,384,256]{2,1,0:T(8,128)(2,1)}, u32[]{:S(2)}, u32[]{:S(2)}) async-start(bf16[8,384,256]{2,1,0:T(8,128)(2,1)} %bitcast.250), calls=%async_computation.3 | async-start | bytes 3145728 | tf_op jit(solution)/shard_map/all_to_all | solution.py:38
  171.3 9.8 %all-to-all-start.4 = ((bf16[1,16,24,256]{3,2,0,1:T(8,128)(2,1)}), bf16[1,16,24,256]{3,2,0,1:T(8,128)(2,1)S(1)}, u32[]{:S(2)}, u32[]{:S(2)}) async-start(bf16[1,16,24,256]{3,2,0,1:T(8,128)(2,1)} %add_convert_fusion), calls=%async_computation.4 | async-start | bytes 393216 | tf_op jit(solution)/shard_map/all_to_all | solution.py:138
  195.4 5.1 %collective-permute-start.7 = (bf16[1,384,256]{2,1,0:T(8,128)(2,1)S(1)}, bf16[1,384,256]{2,1,0:T(8,128)(2,1)S(1)}, u32[]{:S(2)}, u32[]{:S(2)}) collective-permute-start(bf16[1,384,256]{2,1,0:T(8,128)(2,1)S(1)} %bitcast.260), channel_id=1, source_target_pairs={{0,2},{2,4},{4,6},{6,8},{8,10},{10,12},{12,14},{14,0},{1,3},{3,5},... | collective-permute-start | bytes 589832 | tf_op jit(solution)/shard_map/ppermute | solution.py:18
  200.5 5.1 %collective-permute-start.8 = (bf16[1,384,256]{2,1,0:T(8,128)(2,1)S(1)}, bf16[1,384,256]{2,1,0:T(8,128)(2,1)S(1)}, u32[]{:S(2)}, u32[]{:S(2)}) collective-permute-start(bf16[1,384,256]{2,1,0:T(8,128)(2,1)S(1)} %collective-permute-done.7), channel_id=1, source_target_pairs={{0,2},{2,4},{4,6},{6,8},{8,10},{10,12},{12,14},{14,0},{1,3},{3,5},... | collective-permute-start | bytes 589832 | tf_op jit(solution)/shard_map/ppermute | solution.py:18
  200.6 5.1 %collective-permute-start.11 = (bf16[1,384,256]{2,1,0:T(8,128)(2,1)S(1)}, bf16[1,384,256]{2,1,0:T(8,128)(2,1)S(1)}, u32[]{:S(2)}, u32[]{:S(2)}) collective-permute-start(bf16[1,384,256]{2,1,0:T(8,128)(2,1)S(1)} %bitcast.261), channel_id=1, source_target_pairs={{0,14},{2,0},{4,2},{6,4},{8,6},{10,8},{12,10},{14,12},{1,15},{3,1}... | collective-permute-start | bytes 589832 | tf_op jit(solution)/shard_map/ppermute | solution.py:20
  205.6 5.1 %collective-permute-start.9 = (bf16[1,384,256]{2,1,0:T(8,128)(2,1)S(1)}, bf16[1,384,256]{2,1,0:T(8,128)(2,1)S(1)}, u32[]{:S(2)}, u32[]{:S(2)}) collective-permute-start(bf16[1,384,256]{2,1,0:T(8,128)(2,1)S(1)} %collective-permute-done.8), channel_id=1, source_target_pairs={{0,2},{2,4},{4,6},{6,8},{8,10},{10,12},{12,14},{14,0},{1,3},{3,5},... | collective-permute-start | bytes 589832 | tf_op jit(solution)/shard_map/ppermute | solution.py:18
  205.7 5.1 %collective-permute-start.12 = (bf16[1,384,256]{2,1,0:T(8,128)(2,1)S(1)}, bf16[1,384,256]{2,1,0:T(8,128)(2,1)S(1)}, u32[]{:S(2)}, u32[]{:S(2)}) collective-permute-start(bf16[1,384,256]{2,1,0:T(8,128)(2,1)S(1)} %collective-permute-done.11), channel_id=1, source_target_pairs={{0,14},{2,0},{4,2},{6,4},{8,6},{10,8},{12,10},{14,12},{1,15},{3,1}... | collective-permute-start | bytes 589832 | tf_op jit(solution)/shard_map/ppermute | solution.py:20
  210.7 5.1 %collective-permute-start.10 = (bf16[1,384,256]{2,1,0:T(8,128)(2,1)S(1)}, bf16[1,384,256]{2,1,0:T(8,128)(2,1)S(1)}, u32[]{:S(2)}, u32[]{:S(2)}) collective-permute-start(bf16[1,384,256]{2,1,0:T(8,128)(2,1)S(1)} %collective-permute-done.9), channel_id=1, source_target_pairs={{0,2},{2,4},{4,6},{6,8},{8,10},{10,12},{12,14},{14,0},{1,3},{3,5},... | collective-permute-start | bytes 589832 | tf_op jit(solution)/shard_map/ppermute | solution.py:18
  210.8 5.3 %collective-permute-start.13 = (bf16[1,384,256]{2,1,0:T(8,128)(2,1)S(1)}, bf16[1,384,256]{2,1,0:T(8,128)(2,1)S(1)}, u32[]{:S(2)}, u32[]{:S(2)}) collective-permute-start(bf16[1,384,256]{2,1,0:T(8,128)(2,1)S(1)} %collective-permute-done.12), channel_id=1, source_target_pairs={{0,14},{2,0},{4,2},{6,4},{8,6},{10,8},{12,10},{14,12},{1,15},{3,1}... | collective-permute-start | bytes 589832 | tf_op jit(solution)/shard_map/ppermute | solution.py:20
  216.0 2.5 copy-start.15
  216.0 2.5 copy-start.46
  216.3 3.1 copy-start.5
  217.1 4.3 %copy-start.29 = (bf16[384,256]{0,1:T(8,128)(2,1)}, bf16[384,256]{0,1:T(8,128)(2,1)S(1)}, u32[]{:S(2)}) copy-start(bf16[384,256]{0,1:T(8,128)(2,1)S(1)} %fusion.60) | copy-start | bytes 589828
  223.3 4.2 %copy-start.22 = (bf16[64,4,384]{2,0,1:T(8,128)(2,1)S(1)}, bf16[64,4,384]{2,0,1:T(8,128)(2,1)}, u32[]{:S(2)}) copy-start(bf16[64,4,384]{2,0,1:T(8,128)(2,1)} %copy-done.21) | copy-start | bytes 589828
  227.5 3.5 %copy-start.18 = (f32[384,64]{0,1:T(8,128)S(1)}, f32[384,64]{0,1:T(8,128)}, u32[]{:S(2)}) copy-start(f32[384,64]{0,1:T(8,128)} %copy-done.17) | copy-start | bytes 294916
  227.5 3.5 %copy-start.25 = (f32[384,4,64]{0,2,1:T(8,128)S(1)}, f32[384,4,64]{0,2,1:T(8,128)}, u32[]{:S(2)}) copy-start(f32[384,4,64]{0,2,1:T(8,128)} %get-tuple-element.34) | copy-start | bytes 1179652
  227.5 3.5 %copy-start.9 = (bf16[384,2048]{1,0:T(8,128)(2,1)S(1)}, bf16[384,2048]{1,0:T(8,128)(2,1)}, u32[]{:S(2)}) copy-start(bf16[384,2048]{1,0:T(8,128)(2,1)} %param.12) | copy-start | bytes 4718596
  229.8 3.2 %copy-start.24 = (f32[384,32]{0,1:T(8,128)S(1)}, f32[384,32]{0,1:T(8,128)}, u32[]{:S(2)}) copy-start(f32[384,32]{0,1:T(8,128)} %copy-done.23) | copy-start | bytes 147460
  229.8 3.2 %copy-start.34 = (f32[384,64]{0,1:T(8,128)S(1)}, f32[384,64]{0,1:T(8,128)}, u32[]{:S(2)}) copy-start(f32[384,64]{0,1:T(8,128)} %fusion.70) | copy-start | bytes 294916
  229.8 3.2 %copy-start.31 = (f32[384,32]{0,1:T(8,128)S(1)}, f32[384,32]{0,1:T(8,128)}, u32[]{:S(2)}) copy-start(f32[384,32]{0,1:T(8,128)} %copy-done.30) | copy-start | bytes 147460
  233.0 3.3 %copy-start.28 = (bf16[2048,64]{0,1:T(8,128)(2,1)S(1)}, bf16[2048,64]{0,1:T(8,128)(2,1)}, u32[]{:S(2)}) copy-start(bf16[2048,64]{0,1:T(8,128)(2,1)} %convolution_convert_fusion.3) | copy-start | bytes 786436
  (17 other events, 26.9 us)
